TPU v7x, 512 devices: a 8x2x16 block of a 8x8x16 slice. The times are simulated.
512 devices in a mesh: grp: 2 (over y), tx: 16 (over z), ty: 16 (over x, core).
Axes of the slice: x: 8, y: 2, z: 16, core: 2. Of those that a mesh axis runs over, the one named last changes fastest.
The devices are a block of a 8x8x16 slice.
Arguments:
- obj_field: float32 [2, 4096, 2048], P(None, ('grp', 'tx'), 'ty'), parts along dimension 1, may hold values from -6 to 6
- eigenprobes: bfloat16 [2, 32, 128, 128], P(None, 'grp'), parts along dimension 1, may hold values from -1.5 to 1.5
- weights: float32 [32, 16, 3, 16], P(('grp', 'tx'), 'ty'), parts along dimension 0, may hold values from -4 to 4
- offsets: int32 [32, 16, 3, 2], P(('grp', 'tx'), 'ty'), parts along dimension 0, may hold values from 0 to 127
- counts: int32 [32, 16], P(('grp', 'tx'), 'ty'), parts along dimension 0, may hold values from 1 to 3, as said below
- amplitudes: bfloat16 [32, 16, 3, 128, 128], P(('grp', 'tx'), 'ty'), parts along dimension 0, may hold values from 0.19921875 to 3
Outputs:
- new_object: float32 [2, 4096, 2048], P(None, ('grp', 'tx'), 'ty'), parts along dimension 1
- new_eigenprobes: float32 [2, 32, 128, 128], P(None, 'grp'), parts along dimension 1
There are 2 independent parts, one for each index of `grp`. A program takes and returns all parts, laid end to end along the dimension named above; each array names one. Nothing has to cross between parts.
Inputs may be any that keep to these rules, and one draw needn't show every extreme that they name: Every tile holds 1 to 3 positions; some tile holds exactly 3; slots from counts on are unused.
All inputs are finite; a program needn't handle non-finite values.
Results may differ from a plain program's by a relative error of at most 0.0003.
Values sent between devices are 32-bit elements; how exact they have to be, the bound alone decides.
No kernel may reach another device: no remote copies, remote signals or barrier semaphores. Data moves between devices by JAX's collectives and lax.ppermute only.
A program may use at most 64 MiB of HBM per device.

v0:
```python
import functools
import math
import jax
import jax.numpy as jnp
from jax import lax
from jax.sharding import Mesh
from jax.sharding import PartitionSpec as P

TY = ("ty_0", "ty_1")
TX_TY = ("tx", "ty_0", "ty_1")
high = lax.Precision.HIGHEST


def from_behind(value, axis, steps):
    count = lax.axis_size(axis)
    pairs = [(source, (source + steps) % count) for source in range(count)]
    return lax.ppermute(value, axis, pairs)


def one_axis_at_a_time(shard, axes):
    return functools.reduce(lax.psum, axes, shard)


def in_blocks(shard, dim, count):
    before, after = (shard.shape[:dim], shard.shape[dim + 1 :])
    return jnp.moveaxis(shard.reshape(*before, count, -1, *after), dim, 0)


def sent_and_summed(shard, axis, dim):
    tiles = in_blocks(shard, dim, lax.axis_size(axis))
    arrived = lax.all_to_all(tiles, axis, split_axis=0, concat_axis=0, tiled=True)
    return arrived.sum(axis=0)


def gathered_total(shard, axis):
    return lax.all_gather(shard, axis).sum(0)


def tables(frame, sign):
    grid = jnp.arange(frame, dtype=jnp.int32)
    phase = grid[:, None] * grid[None, :] % frame
    angle = phase.astype(jnp.float32) * (2.0 * math.pi / frame)
    scale = 1.0 / math.sqrt(frame)
    return (jnp.cos(angle) * scale, sign * jnp.sin(angle) * scale)


def transform(real_part, imag_part, table_re, table_im):
    left_re = jnp.einsum("jk,skl->sjl", table_re, real_part, precision=high) - jnp.einsum(
        "jk,skl->sjl", table_im, imag_part, precision=high
    )
    left_im = jnp.einsum("jk,skl->sjl", table_re, imag_part, precision=high) + jnp.einsum(
        "jk,skl->sjl", table_im, real_part, precision=high
    )
    out_re = jnp.einsum("sjk,kl->sjl", left_re, table_re, precision=high) - jnp.einsum(
        "sjk,kl->sjl", left_im, table_im, precision=high
    )
    out_im = jnp.einsum("sjk,kl->sjl", left_re, table_im, precision=high) + jnp.einsum(
        "sjk,kl->sjl", left_im, table_re, precision=high
    )
    return (out_re, out_im)


def row_divisor(norms, start, count, frame, modes):
    mode_of_row = (start + jnp.arange(count, dtype=jnp.int32)) // frame % modes
    match = mode_of_row[:, None] == jnp.arange(modes, dtype=jnp.int32)[None, :]
    return jnp.sum(jnp.where(match, norms[None, :] + 1.0, 0.0), axis=1)


def per_device(obj_field, eigenprobes, weights, offsets, counts, amplitudes):
    tile = obj_field.shape[1]
    modes = eigenprobes.shape[1]
    frame = eigenprobes.shape[2]
    slots = weights.shape[2]
    wts = weights[0, 0]
    offs = offsets[0, 0]
    live = (jnp.arange(slots, dtype=jnp.int32) < counts[0, 0]).astype(jnp.float32)
    local_norms = jnp.sum(live[:, None] * wts * wts, axis=0)
    below = from_behind(obj_field, "tx", -1)
    tall = jnp.concatenate([obj_field, below], axis=1)
    beside = from_behind(tall, TY, -1)
    region = jnp.concatenate([tall, beside], axis=2)
    zero_index = jnp.int32(0)

    def read_window(row_start, col_start):
        return lax.dynamic_slice(region, (zero_index, row_start, col_start), (2, frame, frame))

    windows = jax.vmap(read_window)(offs[:, 0], offs[:, 1])
    win_re = windows[:, 0]
    win_im = windows[:, 1]
    eig32 = eigenprobes.astype(jnp.float32)
    probe = jnp.einsum("sk,ckij->csij", wts, eig32, precision=high)
    psi_re = probe[0] * win_re - probe[1] * win_im
    psi_im = probe[0] * win_im + probe[1] * win_re
    fwd_re, fwd_im = tables(frame, -1.0)
    spec_re, spec_im = transform(psi_re, psi_im, fwd_re, fwd_im)
    amps = amplitudes[0, 0].astype(jnp.float32)
    factor = (amps / jnp.sqrt(spec_re * spec_re + spec_im * spec_im + 0.25) - 1.0) * live[
        :, None, None
    ]
    inv_re, inv_im = tables(frame, 1.0)
    chi_re, chi_im = transform(spec_re * factor, spec_im * factor, inv_re, inv_im)
    obj_re = probe[0] * chi_re + probe[1] * chi_im
    obj_im = probe[0] * chi_im - probe[1] * chi_re
    power = (probe[0] * probe[0] + probe[1] * probe[1]) * live[:, None, None]
    pieces = jnp.stack([obj_re, obj_im, power], axis=1)

    def add_slot(slot, acc):
        row_start = offs[slot, 0]
        col_start = offs[slot, 1]
        piece = lax.dynamic_index_in_dim(pieces, slot, 0, keepdims=False)
        current = lax.dynamic_slice(acc, (zero_index, row_start, col_start), (3, frame, frame))
        return lax.dynamic_update_slice(acc, current + piece, (zero_index, row_start, col_start))

    acc = jnp.zeros((3, tile + frame, tile + frame), jnp.float32)
    acc = lax.fori_loop(0, slots, add_slot, acc)
    grad_re = win_re * chi_re + win_im * chi_im
    grad_im = win_re * chi_im - win_im * chi_re
    slot_grad = jnp.stack([grad_re, grad_im])
    spilled = from_behind(acc[:, :, tile:], TY, 1)
    merged = acc[:, :, :tile].at[:, :, :frame].add(spilled)
    dropped = from_behind(merged[:, tile:, :], "tx", 1)
    totals = merged[:, :tile, :].at[:, :frame, :].add(dropped)
    local_illum = jnp.sum(totals[2])
    norms, illum_sum = (
        one_axis_at_a_time(local_norms, TX_TY),
        one_axis_at_a_time(local_illum, TX_TY),
    )
    cells = lax.axis_size("tx") * lax.axis_size(TY) * tile * tile
    mean_illum = illum_sum / cells
    new_object = obj_field + totals[:2] / (totals[2] + mean_illum)[None]
    flat_rows = 2 * modes * frame
    flat_eig = eig32.reshape(flat_rows, frame)
    gprobe = jnp.einsum("sk,csij->ckij", wts, slot_grad, precision=high)
    flat_grad = gprobe.reshape(flat_rows, frame)
    share_rows = flat_rows // lax.axis_size("tx")
    start = lax.axis_index("tx") * share_rows
    partial_value = sent_and_summed(flat_grad, "tx", 0)
    share = gathered_total(partial_value, TY)
    own = lax.dynamic_slice_in_dim(flat_eig, start, share_rows, 0)
    updated = own + share / row_divisor(norms, start, share_rows, frame, modes)[:, None]
    new_eig = lax.all_gather(updated, "tx", axis=0, tiled=True).reshape(2, modes, frame, frame)
    return (new_object, new_eig)


def solution(mesh):
    finer = Mesh(
        mesh.devices.reshape(mesh.shape["grp"], mesh.shape["tx"], 8, 2),
        ("grp", "tx", "ty_0", "ty_1"),
    )
    return jax.shard_map(
        per_device,
        mesh=finer,
        in_specs=(
            P(None, ("grp", "tx"), TY),
            P(None, "grp", None, None),
            P(("grp", "tx"), TY, None, None),
            P(("grp", "tx"), TY, None, None),
            P(("grp", "tx"), TY),
            P(("grp", "tx"), TY, None, None, None),
        ),
        out_specs=(P(None, ("grp", "tx"), TY), P(None, "grp", None, None)),
        check_vma=False,
    )
```

profile of v0, /device:TPU:66, one launch (start us, length us, event | category | flops | bytes accessed | tf_op | source)
XLA Modules:
  0.0 368.5 jit_solution(7381467266140601053)
XLA Ops:
  7.2 44.0 %collective-permute-start = (f32[2,128,128]{2,1,0:T(8,128)}, f32[2,128,128]{2,1,0:T(8,128)S(1)}, u32[]{:S(2)}, u32[]{:S(2)}) collective-permute-start(f32[2,128,128]{2,1,0:T(8,128)} %param.16), channel_id=1, source_target_pairs={{0,240},{16,0},{32,16},{48,32},{64,48},{80,64},{96,80},{112,96},{1... | collective-permute-start | bytes 393224 | tf_op jit(solution)/shard_map/ppermute | solution.py:17
  51.9 0.8 compare_select_fusion.1
  52.8 0.9 constant_dynamic-update-slice_fusion.1
  53.7 0.7 collective-permute-done
  54.5 2.2 convolution_bitcast_fusion.1
  56.7 1.7 collective-permute-done.1
  58.4 15.2 %while.19 = (s32[]{:T(128)}, f32[2,256,256]{2,1,0:T(8,128)S(1)}, s32[3,3]{1,0:T(4,128)S(1)}, f32[3,2,128,128]{3,0,2,1:T(4,128)S(1)}, s32[]{:T(128)}, /*index=5*/s32[]{:T(128)}) while((s32[]{:T(128)}, f32[2,256,256]{2,1,0:T(8,128)S(1)}, s32[3,3]{1,0:T(4,128)S(1)}, f32[3,2,128,128]{3,0,2,1:T(4,128)S(1)}, s32[]{:T(128)}, /*index=5*/s32[]{:T(128)}) %tuple.75), condition=%wide.while_cond.2, body=%wide.while_body.2.sunk | while | flops 2 | bytes 524421 | solution.py:85
  58.4 0.6 fusion.181
  59.0 1.3 constant_dynamic-slice_fusion.12
  60.3 3.1 dynamic-update-slice.11
  63.4 0.6 fusion.181
  64.0 1.3 constant_dynamic-slice_fusion.12
  65.3 3.1 dynamic-update-slice.11
  68.4 0.6 fusion.181
  69.0 1.3 constant_dynamic-slice_fusion.12
  70.3 3.1 dynamic-update-slice.11
  73.6 0.1 fusion.9
  73.7 0.1 copy.63
  73.9 0.6 fusion.50
  74.6 0.6 fusion.46
  75.2 0.6 fusion.3
  75.8 0.7 fusion.32
  76.4 0.6 fusion.48
  77.1 0.6 fusion.2
  77.6 0.6 convolution_add_fusion.1
  78.3 0.6 convolution_subtract_fusion.1
  79.0 0.7 fusion.39
  79.7 0.7 fusion.43
  80.5 0.8 fusion
  81.2 0.7 fusion.28
  81.9 0.6 fusion.37
  82.5 0.8 fusion.1
  83.3 0.6 fusion.41
  84.0 0.7 fusion.26
  84.6 0.6 fusion.11
  85.3 2.1 convolution_bitcast_fusion
  87.4 0.6 copy.84
  88.0 98.6 %all_to_all.5 = f32[16,256,128]{2,1,0:T(8,128)S(1)} all-to-all(f32[16,256,128]{2,1,0:T(8,128)S(1)} %bitcast.175), channel_id=1, replica_groups=mesh['grp'=2,'tx'=16,'ty_0'=8,'ty_1'=2] {'tx'}, dimensions={0} | all-to-all | bytes 4194304 | tf_op jit(solution)/shard_map/all_to_all | solution.py:31
  186.6 0.8 reduce_sum.46
  187.6 0.2 pad_maximum_fusion
  187.9 0.2 copy-done.2
  188.0 22.8 %while.18 = (s32[]{:T(128)}, f32[3,256,256]{2,1,0:T(8,128)S(1)}, s32[3,2]{0,1:T(2,128)S(1)}, f32[3,3,128,128]{3,0,2,1:T(4,128)S(1)}, s32[]{:T(128)}, /*index=5*/s32[]{:T(128)}, s32[]{:T(128)}) while((s32[]{:T(128)}, f32[3,256,256]{2,1,0:T(8,128)S(1)}, s32[3,2]{0,1:T(2,128)S(1)}, f32[3,3,128,128]{3,0,2,1:T(4,128)S(1)}, s32[]{:T(128)}, ...), condition=%wide.region_1.2_spmd, body=%wide.region_0.0_spmd.sunk | while | flops 49160 | bytes 1376445 | solution.py:115
  188.0 0.2 constant_dynamic-slice_fusion.9
  188.2 0.6 constant_dynamic-slice_fusion.10
  192.7 2.9 dynamic_update_slice.8
  195.6 0.2 constant_dynamic-slice_fusion.9
  195.8 0.6 constant_dynamic-slice_fusion.10
  200.2 2.9 dynamic_update_slice.8
  203.1 0.2 constant_dynamic-slice_fusion.9
  203.3 0.6 constant_dynamic-slice_fusion.10
  207.8 3.0 dynamic_update_slice.8
  210.9 3.6 collective-permute-start.2
  214.4 6.8 %collective-permute-done.2 = f32[3,256,128]{2,1,0:T(8,128)S(1)} collective-permute-done((f32[3,256,128]{2,1,0:T(8,128)S(1)}, f32[3,256,128]{2,1,0:T(8,128)S(1)}, u32[]{:S(2)}, u32[]{:S(2)}) %collective-permute-start.2) | collective-permute-done | bytes 393248 | tf_op jit(solution)/shard_map/ppermute | solution.py:17
  221.3 3.6 collective-permute-start.3
  225.1 5.6 %collective-permute-done.3 = f32[3,128,128]{2,1,0:T(8,128)S(1)} collective-permute-done((f32[3,128,128]{2,1,0:T(8,128)S(1)}, f32[3,128,128]{2,1,0:T(8,128)S(1)}, u32[]{:S(2)}, u32[]{:S(2)}) %collective-permute-start.3) | collective-permute-done | bytes 196640 | tf_op jit(solution)/shard_map/ppermute | solution.py:17
  230.8 0.6 slice_reduce_fusion
  231.4 31.6 %all-reduce = (f32[]{:T(128)}, f32[16]{0:T(128)S(1)}) all-reduce(f32[]{:T(128)} %slice_reduce_fusion, f32[16]{0:T(128)S(1)} %fusion.80), channel_id=1, replica_groups=mesh['grp'=2,'tx'=16,'ty_0'=8,'ty_1'=2] {'tx'}, use_global_device_ids=true, to_apply=%region_3.4 | all-reduce | flops 17 | bytes 136 | tf_op jit(solution)/shard_map/psum | solution.py:21
  263.0 20.4 %all-reduce.1 = (f32[]{:T(128)}, f32[16]{0:T(128)S(1)}) all-reduce(f32[]{:T(128)} %get-tuple-element.170, f32[16]{0:T(128)S(1)} %get-tuple-element.171), channel_id=1, replica_groups=mesh['grp'=2,'tx'=16,'ty_0'=8,'ty_1'=2] {'ty_0'}, use_global_device_ids=true, to_apply=%region_4.5 | all-reduce | flops 17 | bytes 136 | tf_op jit(solution)/shard_map/psum | solution.py:21
  283.4 3.1 all-reduce.2
  286.7 1.7 reduce_sum.47
  288.4 1.6 convert_add_fusion
  290.7 0.7 fusion.22
  291.3 67.1 %all-gather.4.cloned.1.call-done = f32[4096,128]{1,0:T(8,128)} async-done(((f32[256,128]{1,0:T(8,128)}), f32[4096,128]{1,0:T(8,128)}) %all-gather.4.cloned.1.call-update) | async-done | bytes 2097168 | tf_op jit(solution)/shard_map/all_gather | solution.py:141
  358.5 3.1 copy.171
  (38 shorter events, 1.5 us)
Async XLA Ops:
  7.2 279.5 %all-gather.6.cloned.1.call-start = ((), (), s32[]{:S(2)}) async-start(), calls=%async_computation.2 | async-start | bytes 2228224 | tf_op jit(solution)/shard_map/all_gather | solution.py:36
  7.2 47.1 %collective-permute-start = (f32[2,128,128]{2,1,0:T(8,128)}, f32[2,128,128]{2,1,0:T(8,128)S(1)}, u32[]{:S(2)}, u32[]{:S(2)}) collective-permute-start(f32[2,128,128]{2,1,0:T(8,128)} %param.16), channel_id=1, source_target_pairs={{0,240},{16,0},{32,16},{48,32},{64,48},{80,64},{96,80},{112,96},{1... | collective-permute-start | bytes 393224 | tf_op jit(solution)/shard_map/ppermute | solution.py:17
  54.4 4.0 %collective-permute-start.1 = (f32[2,256,128]{2,1,0:T(8,128)S(1)}, f32[2,256,128]{2,1,0:T(8,128)S(1)}, u32[]{:S(2)}, u32[]{:S(2)}) collective-permute-start(f32[2,256,128]{2,1,0:T(8,128)S(1)} %constant_dynamic-update-slice_fusion), channel_id=1, source_target_pairs={{0,15},{1,0},{2,1},{3,2},{4,3},{5,4},{6,5},{7,6},{8,7},{9,8},{10,9... | collective-permute-start | bytes 786440 | tf_op jit(solution)/shard_map/ppermute | solution.py:17
  74.4 4.5 %copy-start.1 = (bf16[1,1,3,128,128]{4,3,2,1,0:T(8,128)(2,1)S(1)}, bf16[1,1,3,128,128]{4,3,2,1,0:T(8,128)(2,1)}, u32[]{:S(2)}) copy-start(bf16[1,1,3,128,128]{4,3,2,1,0:T(8,128)(2,1)} %param.21) | copy-start | bytes 294916
  82.5 2.7 copy-start.3
  187.4 0.7 copy-start.2
  187.4 171.0 %all-gather.4.cloned.1.call-start = ((), (), s32[]{:S(2)}) async-start(), calls=%async_computation.1 | async-start | bytes 2228224 | tf_op jit(solution)/shard_map/all_gather | solution.py:141
  210.9 10.4 %collective-permute-start.2 = (f32[3,256,128]{2,1,0:T(8,128)S(1)}, f32[3,256,128]{2,1,0:T(8,128)S(1)}, u32[]{:S(2)}, u32[]{:S(2)}) collective-permute-start(f32[3,256,128]{2,1,0:T(8,128)S(1)} %slice.92), channel_id=1, source_target_pairs={{0,1},{1,2},{2,3},{3,4},{4,5},{5,6},{6,7},{7,8},{8,9},{9,10},{10,1... | collective-permute-start | bytes 1179656 | tf_op jit(solution)/shard_map/ppermute | solution.py:17
  221.3 69.4 %copy-start = (f32[2,128,128]{2,1,0:T(8,128)S(1)}, f32[2,128,128]{2,1,0:T(8,128)}, u32[]{:S(2)}) copy-start(f32[2,128,128]{2,1,0:T(8,128)} %param.16) | copy-start | bytes 393220
  221.3 9.4 %collective-permute-start.3 = (f32[3,128,128]{2,1,0:T(8,128)S(1)}, f32[3,128,128]{2,1,0:T(8,128)S(1)}, u32[]{:S(2)}, u32[]{:S(2)}) collective-permute-start(f32[3,128,128]{2,1,0:T(8,128)S(1)} %slice.115), channel_id=1, source_target_pairs={{0,16},{16,32},{32,48},{48,64},{64,80},{80,96},{96,112},{112,128},... | collective-permute-start | bytes 589832 | tf_op jit(solution)/shard_map/ppermute | solution.py:17
Sparse Core Ops, SparseCore 0:
  187.5 45.9 all-gather.5
  290.2 68.2 all-gather.3
where the time goes:
time: 369 us; the launch traced here: 368 us
  blocking collectives  154 us (42%)
  waiting for transfers between devices  82 us (22%)
  starting transfers between devices  51.5 us (14%)
  local copies, waits for them, and re-layouts  31.5 us (9%)
  between operations  15.7 us (4%)
  matrix products  14.7 us (4%)
  loops' own time  11.4 us (3%)
  other arithmetic  7.88 us (2%)
    all_to_all x1, blocking collectives, sent_and_summed(): lax.all_to_all(tiles, axis, split_axis=0, concat_axis=0, tiled=True)  98.6 us
    all_gather x1, waiting for transfers between devices, per_device(): lax.all_gather(updated, 'tx', axis=0, tiled=True)  67.1 us
    psum x3, blocking collectives, one_axis_at_a_time(): return functools.reduce(lax.psum, axes, shard)  55.2 us
    ppermute x4, starting transfers between devices, from_behind(): return lax.ppermute(value, axis, pairs)  51.3 us
    gather x12, local copies, waits for them, and re-layouts  14.9 us
    ppermute x4, waiting for transfers between devices, from_behind(): return lax.ppermute(value, axis, pairs)  14.8 us
    another operation x1, loops' own time, per_device(): acc = lax.fori_loop(0, slots, add_slot, acc)  11.1 us
    dynamic_update_slice x3, local copies, waits for them, and re-layouts, add_slot(): lax.dynamic_update_slice(acc, current + piece, (zero_index, row_start, co...  8.83 us
  transfers between devices with their start and end apart: 6, of which 5 were waited for; matrix products, arithmetic and copies ran while one was open for 5% of the time, Pallas kernels for 0%

commit v1 on v0

--- a/solution.py
+++ b/solution.py
@@ -9,6 +9,14 @@
 TY = ("ty_0", "ty_1")
 TX_TY = ("tx", "ty_0", "ty_1")
 high = lax.Precision.HIGHEST
+
+
+def gather_from_all(value, axis, dim):
+    size = lax.axis_size(axis)
+    repeats = [size if d == dim else 1 for d in range(value.ndim)]
+    return lax.all_to_all(
+        jnp.tile(value, repeats), axis, split_axis=dim, concat_axis=dim, tiled=True
+    )
 
 
 def from_behind(value, axis, steps):
@@ -138,7 +146,7 @@
     share = gathered_total(partial_value, TY)
     own = lax.dynamic_slice_in_dim(flat_eig, start, share_rows, 0)
     updated = own + share / row_divisor(norms, start, share_rows, frame, modes)[:, None]
-    new_eig = lax.all_gather(updated, "tx", axis=0, tiled=True).reshape(2, modes, frame, frame)
+    new_eig = gather_from_all(updated, "tx", 0).reshape(2, modes, frame, frame)
     return (new_object, new_eig)
 
 

time: 369 us -> 401 us (1.087)
  the two profiles are of different devices: /device:TPU:66 before, /device:TPU:80 now
where the time goes in v1:
time: 401 us; the launch traced here: 400 us
  blocking collectives  149 us (37%)
  waiting for transfers between devices  115 us (29%)
  starting transfers between devices  55.9 us (14%)
  local copies, waits for them, and re-layouts  31.7 us (8%)
  between operations  15.7 us (4%)
  matrix products  14.7 us (4%)
  loops' own time  11.4 us (3%)
  other arithmetic  7.22 us (2%)
    all_to_all x1, blocking collectives, sent_and_summed(): lax.all_to_all(tiles, axis, split_axis=0, concat_axis=0, tiled=True)  101 us
    all_to_all x1, waiting for transfers between devices, gather_from_all(): lax.all_to_all(jnp.tile(value, repeats), axis, split_axis=dim, concat_axi...  93.6 us
    ppermute x4, starting transfers between devices, from_behind(): return lax.ppermute(value, axis, pairs)  50 us
    psum x3, blocking collectives, one_axis_at_a_time(): return functools.reduce(lax.psum, axes, shard)  48.1 us
    ppermute x4, waiting for transfers between devices, from_behind(): return lax.ppermute(value, axis, pairs)  21 us
    gather x12, local copies, waits for them, and re-layouts  15.5 us
    another operation x1, loops' own time, per_device(): acc = lax.fori_loop(0, slots, add_slot, acc)  11.1 us
    dynamic_update_slice x3, local copies, waits for them, and re-layouts, add_slot(): lax.dynamic_update_slice(acc, current + piece, (zero_index, row_start, co...  8.6 us
  transfers between devices with their start and end apart: 6, of which 5 were waited for; matrix products, arithmetic and copies ran while one was open for 4% of the time, Pallas kernels for 0%

profile of v1, /device:TPU:80, one launch (start us, length us, event | category | flops | bytes accessed | tf_op | source)
XLA Modules:
  0.0 400.1 jit_solution(12546892815534305653)
XLA Ops:
  7.2 44.0 %collective-permute-start = (f32[2,128,128]{2,1,0:T(8,128)}, f32[2,128,128]{2,1,0:T(8,128)S(1)}, u32[]{:S(2)}, u32[]{:S(2)}) collective-permute-start(f32[2,128,128]{2,1,0:T(8,128)} %param.16), channel_id=1, source_target_pairs={{0,240},{16,0},{32,16},{48,32},{64,48},{80,64},{96,80},{112,96},{1... | collective-permute-start | bytes 393224 | tf_op jit(solution)/shard_map/ppermute | solution.py:25
  51.9 0.8 compare_select_fusion.1
  52.8 0.9 constant_dynamic-update-slice_fusion.1
  53.7 0.7 collective-permute-done
  54.4 2.5 collective-permute-start.1
  56.9 2.2 convolution_bitcast_fusion.1
  59.1 1.7 collective-permute-done.1
  60.9 15.8 %while.19 = (s32[]{:T(128)}, f32[2,256,256]{2,1,0:T(8,128)S(1)}, s32[3,3]{1,0:T(4,128)S(1)}, f32[3,2,128,128]{3,0,2,1:T(4,128)S(1)}, s32[]{:T(128)}, /*index=5*/s32[]{:T(128)}) while((s32[]{:T(128)}, f32[2,256,256]{2,1,0:T(8,128)S(1)}, s32[3,3]{1,0:T(4,128)S(1)}, f32[3,2,128,128]{3,0,2,1:T(4,128)S(1)}, s32[]{:T(128)}, /*index=5*/s32[]{:T(128)}) %tuple.75), condition=%wide.while_cond.2, body=%wide.while_body.2.sunk | while | flops 2 | bytes 524421 | solution.py:93
  60.9 0.7 fusion.181
  61.6 1.4 constant_dynamic-slice_fusion.12
  63.0 3.1 dynamic-update-slice.11
  66.1 0.7 fusion.181
  66.8 1.4 constant_dynamic-slice_fusion.12
  68.2 3.1 dynamic-update-slice.11
  71.3 0.7 fusion.181
  72.0 1.4 constant_dynamic-slice_fusion.12
  73.4 3.1 dynamic-update-slice.11
  77.0 0.6 fusion.50
  77.7 0.6 fusion.46
  78.3 0.6 fusion.3
  78.8 0.7 fusion.32
  79.5 0.6 fusion.48
  80.1 0.6 fusion.2
  80.7 0.7 convolution_add_fusion.1
  81.4 0.7 convolution_subtract_fusion.1
  82.0 0.7 fusion.39
  82.8 0.7 fusion.43
  83.6 0.8 fusion
  84.3 0.7 fusion.28
  85.0 0.6 fusion.37
  85.6 0.7 fusion.1
  86.4 0.6 fusion.41
  87.0 0.7 fusion.26
  87.7 0.6 fusion.11
  88.4 2.1 convolution_bitcast_fusion
  90.5 0.6 copy.84
  91.1 100.8 %all_to_all.11 = f32[16,256,128]{2,1,0:T(8,128)S(1)} all-to-all(f32[16,256,128]{2,1,0:T(8,128)S(1)} %bitcast.176), channel_id=1, replica_groups=mesh['grp'=2,'tx'=16,'ty_0'=8,'ty_1'=2] {'tx'}, dimensions={0} | all-to-all | bytes 4194304 | tf_op jit(solution)/shard_map/all_to_all | solution.py:39
  191.9 0.8 reduce_sum.46
  192.8 0.2 pad_maximum_fusion
  193.0 0.3 copy-done.2
  193.3 22.5 %while.18 = (s32[]{:T(128)}, f32[3,256,256]{2,1,0:T(8,128)S(1)}, s32[3,2]{0,1:T(2,128)S(1)}, f32[3,3,128,128]{3,0,2,1:T(4,128)S(1)}, s32[]{:T(128)}, /*index=5*/s32[]{:T(128)}, s32[]{:T(128)}) while((s32[]{:T(128)}, f32[3,256,256]{2,1,0:T(8,128)S(1)}, s32[3,2]{0,1:T(2,128)S(1)}, f32[3,3,128,128]{3,0,2,1:T(4,128)S(1)}, s32[]{:T(128)}, ...), condition=%wide.region_1.2_spmd, body=%wide.region_0.0_spmd.sunk | while | flops 49160 | bytes 1376445 | solution.py:123
  193.3 0.2 constant_dynamic-slice_fusion.9
  193.5 0.6 constant_dynamic-slice_fusion.10
  197.9 2.8 dynamic_update_slice.8
  200.7 0.2 constant_dynamic-slice_fusion.9
  200.9 0.6 constant_dynamic-slice_fusion.10
  205.4 3.0 dynamic_update_slice.8
  208.4 0.2 constant_dynamic-slice_fusion.9
  208.6 0.6 constant_dynamic-slice_fusion.10
  213.1 2.8 dynamic_update_slice.8
  216.0 11.6 %collective-permute-done.2 = f32[3,256,128]{2,1,0:T(8,128)S(1)} collective-permute-done((f32[3,256,128]{2,1,0:T(8,128)S(1)}, f32[3,256,128]{2,1,0:T(8,128)S(1)}, u32[]{:S(2)}, u32[]{:S(2)}) %collective-permute-start.2) | collective-permute-done | bytes 393248 | tf_op jit(solution)/shard_map/ppermute | solution.py:25
  227.6 3.4 collective-permute-start.3
  231.1 7.1 %collective-permute-done.3 = f32[3,128,128]{2,1,0:T(8,128)S(1)} collective-permute-done((f32[3,128,128]{2,1,0:T(8,128)S(1)}, f32[3,128,128]{2,1,0:T(8,128)S(1)}, u32[]{:S(2)}, u32[]{:S(2)}) %collective-permute-start.3) | collective-permute-done | bytes 196640 | tf_op jit(solution)/shard_map/ppermute | solution.py:25
  238.2 0.6 slice_reduce_fusion
  238.8 29.7 %all-reduce = (f32[]{:T(128)}, f32[16]{0:T(128)S(1)}) all-reduce(f32[]{:T(128)} %slice_reduce_fusion, f32[16]{0:T(128)S(1)} %fusion.80), channel_id=1, replica_groups=mesh['grp'=2,'tx'=16,'ty_0'=8,'ty_1'=2] {'tx'}, use_global_device_ids=true, to_apply=%region_3.4 | all-reduce | flops 17 | bytes 136 | tf_op jit(solution)/shard_map/psum | solution.py:29
  268.4 15.3 %all-reduce.1 = (f32[]{:T(128)}, f32[16]{0:T(128)S(1)}) all-reduce(f32[]{:T(128)} %get-tuple-element.170, f32[16]{0:T(128)S(1)} %get-tuple-element.171), channel_id=1, replica_groups=mesh['grp'=2,'tx'=16,'ty_0'=8,'ty_1'=2] {'ty_0'}, use_global_device_ids=true, to_apply=%region_4.5 | all-reduce | flops 17 | bytes 136 | tf_op jit(solution)/shard_map/psum | solution.py:29
  283.8 3.1 all-reduce.2
  287.0 1.7 reduce_sum.47
  288.7 1.0 convert_add_fusion
  289.7 1.5 tile.2
  291.2 5.8 %all-to-all-start.1 = ((f32[16,256,128]{2,1,0:T(8,128)}), f32[16,256,128]{2,1,0:T(8,128)S(1)}, u32[]{:S(2)}, u32[]{:S(2)}) async-start(f32[16,256,128]{2,1,0:T(8,128)} %tile.2), calls=%async_computation.1 | async-start | bytes 4194304 | tf_op jit(solution)/shard_map/all_to_all | solution.py:17
  297.7 0.7 fusion.22
  298.4 93.6 %all-to-all-done.1 = f32[16,256,128]{2,1,0:T(8,128)S(1)} async-done(((f32[16,256,128]{2,1,0:T(8,128)}), f32[16,256,128]{2,1,0:T(8,128)S(1)}, u32[]{:S(2)}, u32[]{:S(2)}) %all-to-all-start.1) | async-done | bytes 2097184 | tf_op jit(solution)/shard_map/all_to_all | solution.py:17
  391.9 1.3 copy.171
  (38 shorter events, 1.6 us)
Async XLA Ops:
  7.2 279.8 %all-gather.3.cloned.1.call-start = ((), (), s32[]{:S(2)}) async-start(), calls=%async_computation.2 | async-start | bytes 2228224 | tf_op jit(solution)/shard_map/all_gather | solution.py:44
  7.2 47.1 %collective-permute-start = (f32[2,128,128]{2,1,0:T(8,128)}, f32[2,128,128]{2,1,0:T(8,128)S(1)}, u32[]{:S(2)}, u32[]{:S(2)}) collective-permute-start(f32[2,128,128]{2,1,0:T(8,128)} %param.16), channel_id=1, source_target_pairs={{0,240},{16,0},{32,16},{48,32},{64,48},{80,64},{96,80},{112,96},{1... | collective-permute-start | bytes 393224 | tf_op jit(solution)/shard_map/ppermute | solution.py:25
  54.4 6.4 %collective-permute-start.1 = (f32[2,256,128]{2,1,0:T(8,128)S(1)}, f32[2,256,128]{2,1,0:T(8,128)S(1)}, u32[]{:S(2)}, u32[]{:S(2)}) collective-permute-start(f32[2,256,128]{2,1,0:T(8,128)S(1)} %constant_dynamic-update-slice_fusion), channel_id=1, source_target_pairs={{0,15},{1,0},{2,1},{3,2},{4,3},{5,4},{6,5},{7,6},{8,7},{9,8},{10,9... | collective-permute-start | bytes 786440 | tf_op jit(solution)/shard_map/ppermute | solution.py:25
  77.5 4.5 %copy-start.1 = (bf16[1,1,3,128,128]{4,3,2,1,0:T(8,128)(2,1)S(1)}, bf16[1,1,3,128,128]{4,3,2,1,0:T(8,128)(2,1)}, u32[]{:S(2)}) copy-start(bf16[1,1,3,128,128]{4,3,2,1,0:T(8,128)(2,1)} %param.21) | copy-start | bytes 294916
  85.6 2.7 copy-start.3
  192.6 0.7 copy-start.2
  215.9 11.7 %collective-permute-start.2 = (f32[3,256,128]{2,1,0:T(8,128)S(1)}, f32[3,256,128]{2,1,0:T(8,128)S(1)}, u32[]{:S(2)}, u32[]{:S(2)}) collective-permute-start(f32[3,256,128]{2,1,0:T(8,128)S(1)} %slice.92), channel_id=1, source_target_pairs={{0,1},{1,2},{2,3},{3,4},{4,5},{5,6},{6,7},{7,8},{8,9},{9,10},{10,1... | collective-permute-start | bytes 1179656 | tf_op jit(solution)/shard_map/ppermute | solution.py:25
  227.6 10.5 %collective-permute-start.3 = (f32[3,128,128]{2,1,0:T(8,128)S(1)}, f32[3,128,128]{2,1,0:T(8,128)S(1)}, u32[]{:S(2)}, u32[]{:S(2)}) collective-permute-start(f32[3,128,128]{2,1,0:T(8,128)S(1)} %slice.115), channel_id=1, source_target_pairs={{0,16},{16,32},{32,48},{48,64},{64,80},{80,96},{96,112},{112,128},... | collective-permute-start | bytes 589832 | tf_op jit(solution)/shard_map/ppermute | solution.py:25
  291.2 6.5 %copy-start = (f32[2,128,128]{2,1,0:T(8,128)S(1)}, f32[2,128,128]{2,1,0:T(8,128)}, u32[]{:S(2)}) copy-start(f32[2,128,128]{2,1,0:T(8,128)} %param.16) | copy-start | bytes 393220
  291.2 100.8 %all-to-all-start.1 = ((f32[16,256,128]{2,1,0:T(8,128)}), f32[16,256,128]{2,1,0:T(8,128)S(1)}, u32[]{:S(2)}, u32[]{:S(2)}) async-start(f32[16,256,128]{2,1,0:T(8,128)} %tile.2), calls=%async_computation.1 | async-start | bytes 4194304 | tf_op jit(solution)/shard_map/all_to_all | solution.py:17
Sparse Core Ops, SparseCore 0:
  192.8 40.1 all-gather.2
